TPU v7x, 32 devices: a whole 2x2x4 slice. The times are simulated.
32 devices in a mesh: dp: 8 (over z, y), tensor: 4 (over x, core).
Axes of the slice: x: 2, y: 2, z: 4, core: 2. Of those that a mesh axis runs over, the one named last changes fastest.
Arguments:
- tokens: bfloat16 [37632, 768], P(('dp', 'tensor')), may hold values from -21 to 21
- res_class: int32 [192], P('dp'), may hold values from 0 to 1
- gain_attn: float32 [768], replicated, may hold values from 0.5 to 1.5
- shift_attn: float32 [768], replicated, may hold values from -1.5 to 1.5
- w_qkv: bfloat16 [768, 3, 768], P(None, None, 'tensor'), may hold values from -0.3125 to 0.3125
- bias_qv: float32 [2, 768], P(None, 'tensor'), may hold values from -1.5 to 1.5
- w_out: bfloat16 [768, 768], P('tensor'), may hold values from -0.625 to 0.625
- bias_out: float32 [768], replicated, may hold values from -1.5 to 1.5
- gain_mlp: float32 [768], replicated, may hold values from 0.5 to 1.5
- shift_mlp: float32 [768], replicated, may hold values from -1.5 to 1.5
- w_up: bfloat16 [768, 3072], P(None, 'tensor'), may hold values from -0.21875 to 0.21875
- bias_up: float32 [3072], P('tensor'), may hold values from -1.5 to 1.5
- w_down: bfloat16 [3072, 768], P('tensor'), may hold values from -0.15625 to 0.15625
- bias_down: float32 [768], replicated, may hold values from -1.5 to 1.5
- cotangent: bfloat16 [37632, 768], P(('dp', 'tensor')), may hold values from -21 to 21
Outputs:
- block_out: bfloat16 [37632, 768], P(('dp', 'tensor'))
- grad_tokens: float32 [37632, 768], P(('dp', 'tensor'))
- grad_gain_attn: float32 [768], replicated
- grad_shift_attn: float32 [768], replicated
- grad_qkv: float32 [768, 3, 768], P(None, None, 'tensor')
- grad_bias_qv: float32 [2, 768], P(None, 'tensor')
- grad_out: float32 [768, 768], P('tensor')
- grad_bias_out: float32 [768], replicated
- grad_gain_mlp: float32 [768], replicated
- grad_shift_mlp: float32 [768], replicated
- grad_up: float32 [768, 3072], P(None, 'tensor')
- grad_bias_up: float32 [3072], P('tensor')
- grad_down: float32 [3072, 768], P('tensor')
- grad_bias_down: float32 [768], replicated
- rms: float32 [3], replicated
All inputs are finite; a program needn't handle non-finite values.
Results may differ from a plain program's by a relative error of at most 0.017.
Values may be sent and summed in bfloat16 or wider, within the bound.
A program may use at most 256 MiB of HBM per device.

v0:
```python
import jax
import jax.numpy as jnp
from jax import lax
from jax.sharding import PartitionSpec as P

HEAD_DIM = 64
PATCHES = 196
PATCHES_LOW = 144
EPS = 1e-06


def normalize(values):
    mean = jnp.mean(values, axis=-1, keepdims=True)
    centred = values - mean
    factor = lax.rsqrt(jnp.mean(centred * centred, axis=-1, keepdims=True) + EPS)
    return (centred * factor, factor)


def norm_back(grad_out, gain, normed, factor):
    scaled = grad_out * gain
    return factor * (
        scaled
        - jnp.mean(scaled, axis=-1, keepdims=True)
        - normed * jnp.mean(scaled * normed, axis=-1, keepdims=True)
    )


def exact_gelu(values):
    return jax.nn.gelu(values, approximate=False)


def on_device(
    tokens,
    res_class,
    gain_attn,
    shift_attn,
    w_qkv,
    bias_qv,
    w_out,
    bias_out,
    gain_mlp,
    shift_mlp,
    w_up,
    bias_up,
    w_down,
    bias_down,
    cotangent,
):
    rows = tokens.shape[0]
    width = tokens.shape[1]
    images = res_class.shape[0]
    local = w_qkv.shape[2]
    heads_here = local // HEAD_DIM
    scale = HEAD_DIM ** (-0.5)
    place = lax.axis_index("tensor")
    counts = jnp.where(res_class == 0, PATCHES, PATCHES_LOW)
    key_valid = jnp.arange(PATCHES)[None, :] < counts[:, None]
    flat_valid = key_valid.reshape(-1).astype(jnp.float32)
    row_valid = lax.dynamic_slice_in_dim(flat_valid, place * rows, rows)[:, None]
    mask = key_valid[:, None, None, :]
    shape = (images, PATCHES, heads_here, HEAD_DIM)
    w_qkv_flat = w_qkv.reshape(width, 3 * local)
    inputs = tokens.astype(jnp.float32)
    normed_a, factor_a = normalize(inputs)
    in_attn = (normed_a * gain_attn + shift_attn).astype(jnp.bfloat16)
    full_attn = lax.all_gather(in_attn, "tensor", axis=0, tiled=True)
    qkv = jnp.dot(full_attn, w_qkv_flat, preferred_element_type=jnp.float32).reshape(-1, 3, local)
    query = (qkv[:, 0] + bias_qv[0]).astype(jnp.bfloat16).reshape(shape)
    keys = qkv[:, 1].astype(jnp.bfloat16).reshape(shape)
    values = (qkv[:, 2] + bias_qv[1]).astype(jnp.bfloat16).reshape(shape)
    scores = jnp.einsum("iqhd,ikhd->ihqk", query, keys, preferred_element_type=jnp.float32) * scale
    scores = jnp.where(mask, scores, -1e30)
    log_total = jax.nn.logsumexp(scores, axis=-1, keepdims=True)
    probs = jnp.exp(scores - log_total).astype(jnp.bfloat16)
    context = (
        jnp.einsum("ihqk,ikhd->iqhd", probs, values, preferred_element_type=jnp.float32)
        .reshape(-1, local)
        .astype(jnp.bfloat16)
    )
    piece = context
    branch = (
        lax.psum_scatter(
            jnp.dot(piece, w_out, preferred_element_type=jnp.float32).astype(jnp.bfloat16),
            "tensor",
            scatter_dimension=0,
            tiled=True,
        ).astype(jnp.float32)
        + bias_out
    )
    hidden = inputs + branch
    normed_m, factor_m = normalize(hidden)
    in_mlp = (normed_m * gain_mlp + shift_mlp).astype(jnp.bfloat16)
    full_mlp = lax.all_gather(in_mlp, "tensor", axis=0, tiled=True)
    pre_act = jnp.dot(full_mlp, w_up, preferred_element_type=jnp.float32) + bias_up
    act = exact_gelu(pre_act).astype(jnp.bfloat16)
    piece = act
    mlp = (
        lax.psum_scatter(
            jnp.dot(piece, w_down, preferred_element_type=jnp.float32).astype(jnp.bfloat16),
            "tensor",
            scatter_dimension=0,
            tiled=True,
        ).astype(jnp.float32)
        + bias_down
    )
    stream = (hidden + mlp) * row_valid
    block_out = stream.astype(jnp.bfloat16)
    grad_stream = cotangent.astype(jnp.float32) * row_valid
    grad_bias_down = jnp.sum(grad_stream, axis=0)
    grad_mlp_full = lax.all_gather(grad_stream.astype(jnp.bfloat16), "tensor", axis=0, tiled=True)
    weight_down = jnp.einsum("tf,td->fd", act, grad_mlp_full, preferred_element_type=jnp.float32)
    grad_act = jnp.einsum("td,fd->tf", grad_mlp_full, w_down, preferred_element_type=jnp.float32)
    gelu_out, gelu_back = jax.vjp(exact_gelu, pre_act)
    grad_pre = gelu_back(grad_act)[0]
    grad_bias_up = jnp.sum(grad_pre, axis=0)
    grad_pre_low = grad_pre.astype(jnp.bfloat16)
    weight_up = jnp.einsum("td,tf->df", full_mlp, grad_pre_low, preferred_element_type=jnp.float32)
    piece = grad_pre_low
    grad_in_mlp = lax.psum_scatter(
        jnp.einsum("tf,df->td", piece, w_up, preferred_element_type=jnp.float32).astype(
            jnp.bfloat16
        ),
        "tensor",
        scatter_dimension=0,
        tiled=True,
    ).astype(jnp.float32)
    grad_gain_mlp = jnp.sum(grad_in_mlp * normed_m, axis=0)
    grad_shift_mlp = jnp.sum(grad_in_mlp, axis=0)
    grad_hidden = grad_stream + norm_back(grad_in_mlp, gain_mlp, normed_m, factor_m)
    grad_bias_out = jnp.sum(grad_hidden, axis=0)
    grad_branch_full = lax.all_gather(
        grad_hidden.astype(jnp.bfloat16), "tensor", axis=0, tiled=True
    )
    weight_out = jnp.einsum(
        "tc,td->cd", context, grad_branch_full, preferred_element_type=jnp.float32
    )
    grad_context = (
        jnp.einsum("td,cd->tc", grad_branch_full, w_out, preferred_element_type=jnp.float32)
        .astype(jnp.bfloat16)
        .reshape(shape)
    )
    again = jnp.einsum("iqhd,ikhd->ihqk", query, keys, preferred_element_type=jnp.float32) * scale
    again = jnp.where(mask, again, -1e30)
    probs_full = jnp.exp(again - log_total)
    probs_low = probs_full.astype(jnp.bfloat16)
    grad_value = jnp.einsum(
        "ihqk,iqhd->ikhd", probs_low, grad_context, preferred_element_type=jnp.float32
    )
    grad_probs = jnp.einsum(
        "iqhd,ikhd->ihqk", grad_context, values, preferred_element_type=jnp.float32
    )
    row_dot = jnp.sum(probs_full * grad_probs, axis=-1, keepdims=True)
    grad_scores = (probs_full * (grad_probs - row_dot)).astype(jnp.bfloat16)
    grad_query = scale * jnp.einsum(
        "ihqk,ikhd->iqhd", grad_scores, keys, preferred_element_type=jnp.float32
    )
    grad_key = scale * jnp.einsum(
        "ihqk,iqhd->ikhd", grad_scores, query, preferred_element_type=jnp.float32
    )
    query_low = grad_query.reshape(-1, local).astype(jnp.bfloat16)
    key_low = grad_key.reshape(-1, local).astype(jnp.bfloat16)
    value_low = grad_value.reshape(-1, local).astype(jnp.bfloat16)
    grad_bias_qv = jnp.stack(
        [
            jnp.sum(query_low.astype(jnp.float32), axis=0),
            jnp.sum(value_low.astype(jnp.float32), axis=0),
        ]
    )
    grad_qkv_low = jnp.stack([query_low, key_low, value_low], axis=1).reshape(-1, 3 * local)
    weight_qkv = jnp.einsum(
        "td,tc->dc", full_attn, grad_qkv_low, preferred_element_type=jnp.float32
    ).reshape(width, 3, local)
    piece = grad_qkv_low
    grad_in_attn = lax.psum_scatter(
        jnp.einsum("tc,dc->td", piece, w_qkv_flat, preferred_element_type=jnp.float32).astype(
            jnp.bfloat16
        ),
        "tensor",
        scatter_dimension=0,
        tiled=True,
    ).astype(jnp.float32)
    grad_gain_attn = jnp.sum(grad_in_attn * normed_a, axis=0)
    grad_shift_attn = jnp.sum(grad_in_attn, axis=0)
    grad_tokens = grad_hidden + norm_back(grad_in_attn, gain_attn, normed_a, factor_a)
    totals = jnp.stack(
        [
            jnp.sum(stream * stream),
            jnp.sum(branch * branch * row_valid),
            jnp.sum(mlp * mlp * row_valid),
            jnp.sum(row_valid),
        ]
    )
    summed = lax.psum(
        (
            grad_gain_attn,
            grad_shift_attn,
            grad_bias_out,
            grad_gain_mlp,
            grad_shift_mlp,
            grad_bias_down,
            totals,
        ),
        ("dp", "tensor"),
    )
    weight_qkv, grad_bias_qv, weight_out, weight_up, grad_bias_up, weight_down = lax.psum(
        (weight_qkv, grad_bias_qv, weight_out, weight_up, grad_bias_up, weight_down), "dp"
    )
    sums = summed[6]
    rms = jnp.sqrt(sums[:3] / (sums[3] * width))
    return (
        block_out,
        grad_tokens,
        summed[0],
        summed[1],
        weight_qkv,
        grad_bias_qv,
        weight_out,
        summed[2],
        summed[3],
        summed[4],
        weight_up,
        grad_bias_up,
        weight_down,
        summed[5],
        rms,
    )


def solution(mesh):
    in_specs = (
        P(("dp", "tensor"), None),
        P("dp"),
        P(),
        P(),
        P(None, None, "tensor"),
        P(None, "tensor"),
        P("tensor", None),
        P(),
        P(),
        P(),
        P(None, "tensor"),
        P("tensor"),
        P("tensor", None),
        P(),
        P(("dp", "tensor"), None),
    )
    out_specs = (
        P(("dp", "tensor"), None),
        P(("dp", "tensor"), None),
        P(),
        P(),
        P(None, None, "tensor"),
        P(None, "tensor"),
        P("tensor", None),
        P(),
        P(),
        P(),
        P(None, "tensor"),
        P("tensor"),
        P("tensor", None),
        P(),
        P(),
    )
    return jax.shard_map(
        on_device, mesh=mesh, in_specs=in_specs, out_specs=out_specs, check_vma=False
    )
```

profile of v0, /device:TPU:0, one launch (start us, length us, event | category | flops | bytes accessed | tf_op | source)
XLA Modules:
  0.0 985.3 jit_solution(16900257428672392909)
XLA Ops:
  16.8 52.4 %all-gather.5.cloned.1.call-done = bf16[4704,768]{1,0:T(8,128)(2,1)} async-done(((bf16[1176,768]{1,0:T(8,128)(2,1)}), bf16[4704,768]{1,0:T(8,128)(2,1)}) %all-gather.5.cloned.1.call-update) | async-done | bytes 7225360 | tf_op jit(solution)/shard_map/all_gather | solution.py:66
  69.2 7.3 fusion.10
  77.9 3.4 fusion.73
  81.4 6.0 convert_element_type.155
  87.4 6.4 squeeze.9
  93.9 6.4 squeeze.8
  100.3 7.4 fusion.6
  108.3 4.7 exponential_reduce_fusion
  114.0 11.1 %convert_bitcast_fusion = bf16[24,196,3,64]{1,3,2,0:T(8,128)(2,1)S(1)} fusion(f32[24,196,3,64]{1,0,3,2:T(8,128)} %squeeze.8, f32[3,64]{1,0:T(4,128)} %add.138, f32[24,3,196,196]{2,3,1,0:T(8,128)} %copy-done.2, f32[24,3,196]{2,1,0:T(4,128)S(1)} %log_add_fusion, pred[24,196]{1,0:T(8,128)(4,1)S(1)} %get-tuple-element.54), kind=kOutput, calls=%fused_computation.91 | convolution fusion | flops 367815168 | bytes 16544736 | tf_op jit(solution)/shard_map/ihqk,ikhd->iqhd/dot_general | solution.py:76
  127.9 4.7 convert_element_type.159
  132.6 6.5 convolution_convert_fusion.2
  140.7 63.8 %reduce-scatter.5.cloned.1.call-done = bf16[1176,768]{1,0:T(8,128)(2,1)} async-done(((bf16[4704,768]{1,0:T(8,128)(2,1)}), bf16[1176,768]{1,0:T(8,128)(2,1)}) %reduce-scatter.5.cloned.1.call-update) | async-done | bytes 1806352 | tf_op jit(solution)/shard_map/reduce_scatter | solution.py:82
  207.1 4.9 multiply_reduce_fusion.2
  215.4 51.2 %all-gather.7.cloned.1.call-done = bf16[4704,768]{1,0:T(8,128)(2,1)} async-done(((bf16[1176,768]{1,0:T(8,128)(2,1)}), bf16[4704,768]{1,0:T(8,128)(2,1)}) %all-gather.7.cloned.1.call-update) | async-done | bytes 7225360 | tf_op jit(solution)/shard_map/all_gather | solution.py:93
  266.6 11.9 %fusion.74 = f32[4704,768]{1,0:T(8,128)} fusion(bf16[4704,768]{1,0:T(8,128)(2,1)} %all-gather.7.cloned.1.call-done, bf16[768,768]{1,0:T(8,128)(2,1)} %param.25), kind=kOutput, calls=%fused_computation.132 | convolution fusion | flops 5549064192 | bytes 22855680 | tf_op jit(solution)/shard_map/dot_general | solution.py:94
  278.5 41.8 %all-gather.9.cloned.1.call-done = bf16[4704,768]{1,0:T(8,128)(2,1)} async-done(((bf16[1176,768]{1,0:T(8,128)(2,1)}), bf16[4704,768]{1,0:T(8,128)(2,1)}) %all-gather.9.cloned.1.call-update) | async-done | bytes 7225360 | tf_op jit(solution)/shard_map/all_gather | solution.py:110
  320.3 41.0 %fusion.68 = (f32[768]{0:T(1024)S(1)}, bf16[4704,768]{1,0:T(8,128)(2,1)}, f32[4704,768]{1,0:T(8,128)S(1)}) fusion(f32[4704,768]{1,0:T(8,128)} %fusion.74, f32[768]{0:T(1024)S(1)} %copy-done.50, bf16[4704,768]{1,0:T(8,128)(2,1)} %all-gather.9.cloned.1.call-done, bf16[768,768]{1,0:T(8,128)(2,1)S(1)} %copy-done), kind=kOutput, calls=%fused_computation.128 | convolution fusion | flops 5816400896 | bytes 44537856 | tf_op jit(solution)/shard_map/td,fd->tf/dot_general | solution.py:112
  361.3 4.3 multiply_convert_fusion.1
  365.6 10.8 %convolution_convert_fusion.1 = bf16[4704,768]{1,0:T(8,128)(2,1)} fusion(bf16[4704,768]{1,0:T(8,128)(2,1)} %multiply_convert_fusion.1, bf16[768,768]{1,0:T(8,128)(2,1)S(1)} %copy-done), kind=kOutput, calls=%fused_computation.25 | convolution fusion | flops 5552676864 | bytes 15630336 | tf_op jit(solution)/shard_map/dot_general | solution.py:99
  377.7 11.2 %convolution_convert_fusion = bf16[4704,768]{1,0:T(8,128)(2,1)} fusion(bf16[768,768]{1,0:T(8,128)(2,1)S(1)} %copy-done.54, bf16[4704,768]{1,0:T(8,128)(2,1)} %get-tuple-element.43), kind=kOutput, calls=%fused_computation.24 | convolution fusion | flops 5552676864 | bytes 15630336 | tf_op jit(solution)/shard_map/tf,df->td/dot_general | solution.py:120
  389.1 52.8 %reduce-scatter.7.cloned.1.call-done = bf16[1176,768]{1,0:T(8,128)(2,1)} async-done(((bf16[4704,768]{1,0:T(8,128)(2,1)}), bf16[1176,768]{1,0:T(8,128)(2,1)}) %reduce-scatter.7.cloned.1.call-update) | async-done | bytes 1806352 | tf_op jit(solution)/shard_map/reduce_scatter | solution.py:98
  441.8 67.6 %reduce-scatter.9.cloned.1.call-done = bf16[1176,768]{1,0:T(8,128)(2,1)} async-done(((bf16[4704,768]{1,0:T(8,128)(2,1)}), bf16[1176,768]{1,0:T(8,128)(2,1)}) %reduce-scatter.9.cloned.1.call-update) | async-done | bytes 1806352 | tf_op jit(solution)/shard_map/reduce_scatter | solution.py:119
  509.5 8.3 fusion.36
  523.5 51.8 %all-gather.11.cloned.1.call-done = bf16[4704,768]{1,0:T(8,128)(2,1)} async-done(((bf16[1176,768]{1,0:T(8,128)(2,1)}), bf16[4704,768]{1,0:T(8,128)(2,1)}) %all-gather.11.cloned.1.call-update) | async-done | bytes 7225360 | tf_op jit(solution)/shard_map/all_gather | solution.py:131
  575.3 6.8 convolution_convert_fusion.3
  582.1 6.2 reshape.193
  588.3 9.9 %convert_reduce_fusion.3 = (f32[3,64]{1,0:T(4,128)S(1)}, bf16[24,3,64,196]{3,2,1,0:T(8,128)(2,1)}) fusion(f32[24,3,196,196]{2,3,1,0:T(8,128)} %copy-done.2, f32[24,3,196]{2,1,0:T(4,128)S(1)} %copy-done.24, pred[24,196]{1,0:T(8,128)(4,1)S(1)} %copy-done.30, bf16[24,196,3,64]{1,0,3,2:T(8,128)(2,1)} %reshape.193), kind=kOutput, calls=%fused_computation.53 | convolution fusion | flops 367814976 | bytes 14738400 | tf_op jit(solution)/shard_map/ihqk,iqhd->ikhd/dot_general | solution.py:146
  599.8 11.2 %multiply_reduce_fusion = (f32[24,3,196]{2,1,0:T(4,128)S(1)}, f32[24,3,196,196]{2,3,1,0:T(8,128)}) fusion(f32[24,3,196,196]{2,3,1,0:T(8,128)S(1)} %bitcast.79, f32[24,3,196]{2,1,0:T(4,128)S(1)} %copy-done.24, pred[24,196]{1,0:T(8,128)(4,1)S(1)} %copy-done.30, f32[24,196,3,64]{1,0,3,2:T(8,128)} %squeeze.8, f32[3,64]{1,0:T(4,128)S(1)} %copy-done.47, ...), kind=kOutput, calls=%fused_computation.2 | convolution fusion | flops 369663840 | bytes 27664992 | tf_op jit(solution)/shard_map/iqhd,ikhd->ihqk/dot_general | solution.py:149
  611.0 10.2 %multiply_convert_fusion = bf16[24,3,196,196]{2,3,1,0:T(8,128)(2,1)} fusion(f32[24,3,196,196]{2,3,1,0:T(8,128)} %get-tuple-element.59, f32[24,3,196,196]{2,3,1,0:T(8,128)S(1)} %bitcast.79, f32[24,3,196]{2,1,0:T(4,128)S(1)} %get-tuple-element.58, f32[24,3,196]{2,1,0:T(4,128)S(1)} %copy-done.24, pred[24,196]{1,0:T(8,128)(4,1)S(1)} %copy-done.30), kind=kLoop, calls=%fused_computation.1 | loop fusion | flops 16595712 | bytes 27777120 | tf_op jit(solution)/shard_map/convert_element_type | solution.py:153
  621.2 8.7 fusion.43
  630.0 2.9 convert_reduce_fusion.4
  632.9 2.8 copy.53
  635.7 4.7 convert_element_type.185
  643.2 4.7 convert_element_type.179
  647.9 3.0 copy.50
  650.9 3.0 convert_element_type.182
  659.1 7.9 bitcast_convert_fusion
  667.1 11.8 %fusion.38 = f32[768,768]{1,0:T(8,128)} fusion(bf16[4704,768]{1,0:T(8,128)(2,1)} %all-gather.7.cloned.1.call-done, bf16[4704,768]{1,0:T(8,128)(2,1)} %get-tuple-element.43), kind=kOutput, calls=%fused_computation.78 | convolution fusion | flops 5549064192 | bytes 16809984 | tf_op jit(solution)/shard_map/td,tf->df/dot_general | solution.py:117
  678.9 12.2 %fusion.76 = f32[768,768]{1,0:T(8,128)} fusion(bf16[4704,768]{1,0:T(8,128)(2,1)} %multiply_convert_fusion.1, bf16[4704,768]{1,0:T(8,128)(2,1)} %all-gather.9.cloned.1.call-done), kind=kOutput, calls=%fused_computation.134 | convolution fusion | flops 5549064192 | bytes 16809984 | tf_op jit(solution)/shard_map/tf,td->fd/dot_general | solution.py:111
  693.6 5.9 fusion.8
  699.6 2.8 pad_maximum_fusion.1
  702.6 22.3 %all-reduce.1 = (f32[2,192]{1,0:T(2,128)}, f32[768]{0:T(1024)}) all-reduce(f32[2,192]{1,0:T(2,128)S(1)} %pad_maximum_fusion, f32[768]{0:T(1024)S(1)} %get-tuple-element.42), channel_id=1, replica_groups=mesh['dp'=8,'tensor'=4] {'dp'}, use_global_device_ids=true, to_apply=%region_22.23 | all-reduce | flops 1152 | bytes 9216 | tf_op jit(solution)/shard_map/psum | solution.py:205
  724.8 7.6 reduce-scatter.11.cloned.1.call-done
  732.4 3.4 fusion.37
  735.8 44.5 %all-reduce = (f32[768]{0:T(1024)}, f32[768]{0:T(1024)}, f32[768]{0:T(1024)}, f32[768]{0:T(1024)}, f32[768]{0:T(1024)}, /*index=5*/f32[768]{0:T(1024)}, f32[4]{0:T(128)S(1)}) all-reduce(f32[768]{0:T(1024)S(1)} %get-tuple-element.17, f32[768]{0:T(1024)S(1)} %get-tuple-element.25, ...), channel_id=1, replica_groups=mesh['dp'=8,'tensor'=4] {'dp','tensor'}, use_global_device_ids=true, to_apply=%region_16.17 | all-reduce | flops 4612 | bytes 36896 | tf_op jit(solution)/shard_map/psum | solution.py:193
  782.1 4.6 fusion.29
  786.7 183.9 %all-reduce.5.cloned.1.call-done = (f32[768,3,192]{0,2,1:T(8,128)}, f32[192,768]{1,0:T(8,128)}, f32[768,768]{1,0:T(8,128)}, f32[768,768]{1,0:T(8,128)}) async-done(((f32[768,3,192]{0,2,1:T(8,128)}, f32[192,768]{1,0:T(8,128)}, f32[768,768]{1,0:T(8,128)}, f32[768,768]{1,0:T(8,128)}), (f32[768,3,192]{0,2,1:T(8,128)}, f32[192,768]{1,0:T(8,128)}, f32[768,768]{1,0:T(8,128)}, ...) | async-done | bytes 7077904 | tf_op jit(solution)/shard_map/psum | solution.py:205
  970.6 2.9 copy.96
  (194 shorter events, 48.0 us)
Async XLA Ops:
  7.2 313.1 %copy-start = (bf16[768,768]{1,0:T(8,128)(2,1)S(1)}, bf16[768,768]{1,0:T(8,128)(2,1)}, u32[]{:S(2)}) copy-start(bf16[768,768]{1,0:T(8,128)(2,1)} %param.27) | copy-start | bytes 3538948
  7.2 8.9 copy-start.56
  7.2 62.0 %all-gather.5.cloned.1.call-start = ((), (), s32[]{:S(2)}) async-start(), calls=%async_computation.4 | async-start | bytes 9031680 | tf_op jit(solution)/shard_map/all_gather | solution.py:66
  14.7 189.8 %reduce-scatter.5.cloned.1.call-start = ((), (), s32[]{:S(2)}) async-start(), calls=%async_computation.5 | async-start | bytes 9031680 | tf_op jit(solution)/shard_map/reduce_scatter | solution.py:82
  16.8 97.2 %copy-start.29 = (pred[24,196]{1,0:T(8,128)(4,1)}, pred[24,196]{1,0:T(8,128)(4,1)S(1)}, u32[]{:S(2)}) copy-start(pred[24,196]{1,0:T(8,128)(4,1)S(1)} %get-tuple-element.54) | copy-start | bytes 14116
  114.0 11.1 %copy-start.23 = (f32[24,3,196]{2,1,0:T(4,128)}, f32[24,3,196]{2,1,0:T(4,128)S(1)}, u32[]{:S(2)}) copy-start(f32[24,3,196]{2,1,0:T(4,128)S(1)} %log_add_fusion) | copy-start | bytes 169348
  139.1 65.4 %copy-start.41 = (f32[768]{0:T(1024)S(1)}, f32[768]{0:T(1024)}, u32[]{:S(2)}) copy-start(f32[768]{0:T(1024)} %param.22) | copy-start | bytes 9220
  139.1 127.5 %all-gather.7.cloned.1.call-start = ((), (), s32[]{:S(2)}) async-start(), calls=%async_computation.6 | async-start | bytes 9031680 | tf_op jit(solution)/shard_map/all_gather | solution.py:93
  140.7 71.3 %copy-start.37 = (f32[1176]{0:T(1024)}, f32[1176]{0:T(1024)S(1)}, u32[]{:S(2)}) copy-start(f32[1176]{0:T(1024)S(1)} %get-tuple-element.46) | copy-start | bytes 14116
  140.7 71.9 %copy-start.44 = (f32[768]{0:T(1024)S(1)}, f32[768]{0:T(1024)}, u32[]{:S(2)}) copy-start(f32[768]{0:T(1024)} %param.23) | copy-start | bytes 9220
  140.7 71.9 %copy-start.52 = (f32[768]{0:T(1024)S(1)}, f32[768]{0:T(1024)}, u32[]{:S(2)}) copy-start(f32[768]{0:T(1024)} %param.24) | copy-start | bytes 9220
  214.8 105.5 %all-gather.9.cloned.1.call-start = ((), (), s32[]{:S(2)}) async-start(), calls=%async_computation.8 | async-start | bytes 9031680 | tf_op jit(solution)/shard_map/all_gather | solution.py:110
  215.4 104.9 %copy-start.50 = (f32[768]{0:T(1024)S(1)}, f32[768]{0:T(1024)}, u32[]{:S(2)}) copy-start(f32[768]{0:T(1024)} %param.26) | copy-start | bytes 9220
  215.4 226.5 %reduce-scatter.7.cloned.1.call-start = ((), (), s32[]{:S(2)}) async-start(), calls=%async_computation.7 | async-start | bytes 9031680 | tf_op jit(solution)/shard_map/reduce_scatter | solution.py:98
  320.3 41.1 %copy-start.13 = (f32[4704,768]{1,0:T(8,128)S(1)}, f32[4704,768]{1,0:T(8,128)}, u32[]{:S(2)}) copy-start(f32[4704,768]{1,0:T(8,128)} %fusion.74) | copy-start | bytes 43352068
  376.5 133.0 %reduce-scatter.9.cloned.1.call-start = ((), (), s32[]{:S(2)}) async-start(), calls=%async_computation.9 | async-start | bytes 9031680 | tf_op jit(solution)/shard_map/reduce_scatter | solution.py:119
  389.0 120.5 %copy-start.4 = (bf16[1176,768]{1,0:T(8,128)(2,1)S(1)}, bf16[1176,768]{1,0:T(8,128)(2,1)}, u32[]{:S(2)}) copy-start(bf16[1176,768]{1,0:T(8,128)(2,1)} %param.15) | copy-start | bytes 5419012
  389.0 120.5 %copy-start.34 = (f32[1176]{0:T(1024)S(1)}, f32[1176]{0:T(1024)}, u32[]{:S(2)}) copy-start(f32[1176]{0:T(1024)} %copy-done.33) | copy-start | bytes 14116
  389.0 120.5 %copy-start.38 = (f32[1176]{0:T(1024)S(1)}, f32[1176]{0:T(1024)}, u32[]{:S(2)}) copy-start(f32[1176]{0:T(1024)} %copy-done.37) | copy-start | bytes 14116
  389.0 120.5 %copy-start.40 = (f32[1176]{0:T(1024)S(1)}, f32[1176]{0:T(1024)}, u32[]{:S(2)}) copy-start(f32[1176]{0:T(1024)} %copy-done.39) | copy-start | bytes 14116
  389.0 120.5 %copy-start.42 = (f32[768]{0:T(1024)S(1)}, f32[768]{0:T(1024)}, u32[]{:S(2)}) copy-start(f32[768]{0:T(1024)} %param.22) | copy-start | bytes 9220
  389.0 120.5 %copy-start.45 = (f32[768]{0:T(1024)S(1)}, f32[768]{0:T(1024)}, u32[]{:S(2)}) copy-start(f32[768]{0:T(1024)} %param.23) | copy-start | bytes 9220
  389.0 120.5 %copy-start.51 = (f32[768]{0:T(1024)S(1)}, f32[768]{0:T(1024)}, u32[]{:S(2)}) copy-start(f32[768]{0:T(1024)} %param.28) | copy-start | bytes 9220
  389.0 186.2 %all-gather.11.cloned.1.call-start = ((), (), s32[]{:S(2)}) async-start(), calls=%async_computation.10 | async-start | bytes 9031680 | tf_op jit(solution)/shard_map/all_gather | solution.py:131
  520.2 55.1 %copy-start.28 = (bf16[192,768]{1,0:T(8,128)(2,1)S(1)}, bf16[192,768]{1,0:T(8,128)(2,1)}, u32[]{:S(2)}) copy-start(bf16[192,768]{1,0:T(8,128)(2,1)} %param.21) | copy-start | bytes 884740
  523.4 64.8 %copy-start.24 = (f32[24,3,196]{2,1,0:T(4,128)S(1)}, f32[24,3,196]{2,1,0:T(4,128)}, u32[]{:S(2)}) copy-start(f32[24,3,196]{2,1,0:T(4,128)} %copy-done.23) | copy-start | bytes 169348
  523.5 64.8 %copy-start.30 = (pred[24,196]{1,0:T(8,128)(4,1)S(1)}, pred[24,196]{1,0:T(8,128)(4,1)}, u32[]{:S(2)}) copy-start(pred[24,196]{1,0:T(8,128)(4,1)} %copy-done.29) | copy-start | bytes 14116
  523.5 208.9 %reduce-scatter.11.cloned.1.call-start = ((), (), s32[]{:S(2)}) async-start(), calls=%async_computation.11 | async-start | bytes 9031680 | tf_op jit(solution)/shard_map/reduce_scatter | solution.py:174
  582.1 16.2 %slice-start = ((s8[14745600]{0:T(1024)(128)(4,1)}), s8[2162688]{0:T(1024)(128)(4,1)S(1)}, s32[]{:S(2)}) async-start(s8[14745600]{0:T(1024)(128)(4,1)} %bitcast.78), calls=%async_computation.13 | async-start | bytes 4325376
  588.3 10.0 %slice-start.1 = ((s8[14745600]{0:T(1024)(128)(4,1)}), s8[4194304]{0:T(1024)(128)(4,1)S(1)}, s32[]{:S(2)}) async-start(s8[14745600]{0:T(1024)(128)(4,1)} %bitcast.78), calls=%async_computation.14 | async-start | bytes 8388608
  588.3 10.0 %slice-start.2 = ((s8[14745600]{0:T(1024)(128)(4,1)}), s8[4194304]{0:T(1024)(128)(4,1)S(1)}, s32[]{:S(2)}) async-start(s8[14745600]{0:T(1024)(128)(4,1)} %bitcast.78), calls=%async_computation.15 | async-start | bytes 8388608
  588.3 10.9 %slice-start.3 = ((s8[14745600]{0:T(1024)(128)(4,1)}), s8[4194304]{0:T(1024)(128)(4,1)S(1)}, s32[]{:S(2)}) async-start(s8[14745600]{0:T(1024)(128)(4,1)} %bitcast.78), calls=%async_computation.16 | async-start | bytes 8388608
  588.3 11.5 %copy-start.11 = (bf16[24,196,3,64]{1,0,3,2:T(8,128)(2,1)S(1)}, bf16[24,196,3,64]{1,0,3,2:T(8,128)(2,1)}, u32[]{:S(2)}) copy-start(bf16[24,196,3,64]{1,0,3,2:T(8,128)(2,1)} %reshape.193) | copy-start | bytes 5419012
  588.3 11.5 %copy-start.47 = (f32[3,64]{1,0:T(4,128)S(1)}, f32[3,64]{1,0:T(4,128)}, u32[]{:S(2)}) copy-start(f32[3,64]{1,0:T(4,128)} %add.138) | copy-start | bytes 2308
  611.0 10.2 %copy-start.48 = (f32[3,64]{1,0:T(4,128)S(1)}, f32[3,64]{1,0:T(4,128)}, u32[]{:S(2)}) copy-start(f32[3,64]{1,0:T(4,128)} %add.141) | copy-start | bytes 2308
  667.1 303.6 %all-reduce.5.cloned.1.call-start = ((), (), s32[]{:S(2)}) async-start(), calls=%async_computation.12 | async-start | bytes 14155776 | tf_op jit(solution)/shard_map/psum | solution.py:205
  667.1 24.0 %slice-start.8 = ((s8[7225344]{0:T(1024)(128)(4,1)}), s8[4194304]{0:T(1024)(128)(4,1)S(1)}, s32[]{:S(2)}) async-start(s8[7225344]{0:T(1024)(128)(4,1)} %bitcast.86), calls=%async_computation.21 | async-start | bytes 8388608
  667.1 26.5 %slice-start.4 = ((s8[5455872]{0:T(1024)(128)(4,1)}), s8[4194304]{0:T(1024)(128)(4,1)S(1)}, s32[]{:S(2)}) async-start(s8[5455872]{0:T(1024)(128)(4,1)} %bitcast.82), calls=%async_computation.17 | async-start | bytes 8388608
  667.1 26.5 %slice-start.6 = ((s8[7225344]{0:T(1024)(128)(4,1)}), s8[4194304]{0:T(1024)(128)(4,1)S(1)}, s32[]{:S(2)}) async-start(s8[7225344]{0:T(1024)(128)(4,1)} %bitcast.84), calls=%async_computation.19 | async-start | bytes 8388608
  678.9 12.2 %copy-start.14 = (bf16[4704,192]{0,1:T(8,128)(2,1)S(1)}, bf16[4704,192]{0,1:T(8,128)(2,1)}, u32[]{:S(2)}) copy-start(bf16[4704,192]{0,1:T(8,128)(2,1)} %convert_element_type.159) | copy-start | bytes 5419012
  678.9 12.2 %slice-start.9 = ((s8[7225344]{0:T(1024)(128)(4,1)}), s8[3031040]{0:T(1024)(128)(4,1)S(1)}, s32[]{:S(2)}) async-start(s8[7225344]{0:T(1024)(128)(4,1)} %bitcast.86), calls=%async_computation.22 | async-start | bytes 6062080
  678.9 14.7 %slice-start.5 = ((s8[5455872]{0:T(1024)(128)(4,1)}), s8[1261568]{0:T(1024)(128)(4,1)S(1)}, s32[]{:S(2)}) async-start(s8[5455872]{0:T(1024)(128)(4,1)} %bitcast.82), calls=%async_computation.18 | async-start | bytes 2523136
  678.9 14.7 %slice-start.7 = ((s8[7225344]{0:T(1024)(128)(4,1)}), s8[3031040]{0:T(1024)(128)(4,1)S(1)}, s32[]{:S(2)}) async-start(s8[7225344]{0:T(1024)(128)(4,1)} %bitcast.84), calls=%async_computation.20 | async-start | bytes 6062080
  699.5 32.8 %copy-start.5 = (bf16[1176,768]{1,0:T(8,128)(2,1)S(1)}, bf16[1176,768]{1,0:T(8,128)(2,1)}, u32[]{:S(2)}) copy-start(bf16[1176,768]{1,0:T(8,128)(2,1)} %param.15) | copy-start | bytes 5419012
  699.5 32.8 %copy-start.32 = (f32[1176]{0:T(1024)S(1)}, f32[1176]{0:T(1024)}, u32[]{:S(2)}) copy-start(f32[1176]{0:T(1024)} %copy-done.31) | copy-start | bytes 14116
  699.5 32.8 %copy-start.36 = (f32[1176]{0:T(1024)S(1)}, f32[1176]{0:T(1024)}, u32[]{:S(2)}) copy-start(f32[1176]{0:T(1024)} %copy-done.35) | copy-start | bytes 14116
  699.6 32.8 %copy-start.46 = (f32[768]{0:T(1024)S(1)}, f32[768]{0:T(1024)}, u32[]{:S(2)}) copy-start(f32[768]{0:T(1024)} %param.17) | copy-start | bytes 9220
  699.6 36.3 %copy-start.49 = (f32[768]{0:T(1024)S(1)}, f32[768]{0:T(1024)}, u32[]{:S(2)}) copy-start(f32[768]{0:T(1024)} %get-tuple-element.26) | copy-start | bytes 9220
  (28 other events, 124.3 us)
Sparse Core Ops, SparseCore 0:
  14.8 54.3 all-gather.4
  139.3 65.1 reduce-scatter.4
  214.9 51.6 all-gather.6
  268.6 51.6 all-gather.8
  376.6 65.1 reduce-scatter.6
  444.3 65.1 reduce-scatter.8
  523.6 51.6 all-gather.10
  667.2 65.1 reduce-scatter.10
  738.0 232.6 all-reduce.4
where the time goes:
time: 995 us; the launch traced here: 985 us
  waiting for transfers between devices  574 us (58%)
  matrix products  187 us (19%)
  local copies, waits for them, and re-layouts  81.1 us (8%)
  blocking collectives  66.7 us (7%)
  other arithmetic  61.1 us (6%)
  between operations  15.5 us (2%)
    psum x1, waiting for transfers between devices, on_device(): lax.psum((weight_qkv, grad_bias_qv, weight_out, weight_up, grad_bias_up,...  184 us
    reduce_scatter x1, waiting for transfers between devices, on_device(): lax.psum_scatter(jnp.einsum('tf,df->td', piece, w_up, preferred_element_t...  67.6 us
    reduce_scatter x1, waiting for transfers between devices, on_device(): lax.psum_scatter(jnp.dot(piece, w_out, preferred_element_type=jnp.float32...  63.8 us
    reduce_scatter x1, waiting for transfers between devices, on_device(): lax.psum_scatter(jnp.dot(piece, w_down, preferred_element_type=jnp.float3...  52.8 us
    all_gather x1, waiting for transfers between devices, on_device(): full_attn = lax.all_gather(in_attn, 'tensor', axis=0, tiled=True)  52.4 us
    all_gather x1, waiting for transfers between devices, on_device(): lax.all_gather(grad_hidden.astype(jnp.bfloat16), 'tensor', axis=0, tiled=...  51.8 us
    all_gather x1, waiting for transfers between devices, on_device(): full_mlp = lax.all_gather(in_mlp, 'tensor', axis=0, tiled=True)  51.2 us
    psum x1, blocking collectives, on_device(): lax.psum((grad_gain_attn, grad_shift_attn, grad_bias_out, grad_gain_mlp,...  44.5 us
  transfers between devices with their start and end apart: 9, of which 9 were waited for; matrix products, arithmetic and copies ran while one was open for 7% of the time, Pallas kernels for 0%

commit v1 on v0

--- a/solution.py
+++ b/solution.py
@@ -7,6 +7,28 @@
 PATCHES = 196
 PATCHES_LOW = 144
 EPS = 1e-06
+
+
+def laid_out(blocks, dim):
+    blocks = jnp.moveaxis(blocks, 0, dim)
+    shape = blocks.shape
+    return blocks.reshape(*shape[:dim], shape[dim] * shape[dim + 1], *shape[dim + 2 :])
+
+
+def doubled(x, axis):
+    devices = lax.axis_size(axis)
+    tiles = x[None]
+    for level in range(devices.bit_length() - 1):
+        bit = 1 << level
+        other = lax.ppermute(tiles, axis, [(i, i ^ bit) for i in range(devices)])
+        both = jnp.stack([tiles, other])
+        upper = lax.axis_index(axis) >> level & 1
+        tiles = jnp.where(upper == 0, both, both[::-1]).reshape(-1, *x.shape)
+    return tiles
+
+
+def doubled_up(x, axis, dim):
+    return laid_out(doubled(x, axis), dim)
 
 
 def normalize(values):
@@ -63,7 +85,7 @@
     inputs = tokens.astype(jnp.float32)
     normed_a, factor_a = normalize(inputs)
     in_attn = (normed_a * gain_attn + shift_attn).astype(jnp.bfloat16)
-    full_attn = lax.all_gather(in_attn, "tensor", axis=0, tiled=True)
+    full_attn = doubled_up(in_attn, "tensor", 0)
     qkv = jnp.dot(full_attn, w_qkv_flat, preferred_element_type=jnp.float32).reshape(-1, 3, local)
     query = (qkv[:, 0] + bias_qv[0]).astype(jnp.bfloat16).reshape(shape)
     keys = qkv[:, 1].astype(jnp.bfloat16).reshape(shape)

time: 995 us -> 1040 us (1.045)
  waiting for transfers between devices: 574 us -> 603 us
  other arithmetic: 61.1 us -> 76.2 us
    ppermute x0 -> x2, waiting for transfers between devices: none -> 80.4 us  [doubled(): other = lax.ppermute(tiles, axis, [(i, i ^ bit) for i in range(devices)])]
    all_gather x1 -> x0, waiting for transfers between devices: 52.4 us -> none  [on_device(): full_attn = lax.all_gather(in_attn, 'tensor', axis=0, tiled=True)]
    another operation x0 -> x4, other arithmetic: none -> 13.1 us  [doubled(): both = jnp.stack([tiles, other])]
  transfers between devices with their start and end apart: 9 -> 10, of which waited for: 9 -> 10; matrix products, arithmetic and copies ran while one was open for 7% -> 7% of each run, Pallas kernels for 0% -> 0%
where the time goes in v1:
time: 1040 us; the launch traced here: 1030 us
  waiting for transfers between devices  603 us (58%)
  matrix products  187 us (18%)
  local copies, waits for them, and re-layouts  80.6 us (8%)
  other arithmetic  76.2 us (7%)
  blocking collectives  66.7 us (6%)
  between operations  15.6 us (2%)
    psum x1, waiting for transfers between devices, on_device(): lax.psum((weight_qkv, grad_bias_qv, weight_out, weight_up, grad_bias_up,...  184 us
    ppermute x2, waiting for transfers between devices, doubled(): other = lax.ppermute(tiles, axis, [(i, i ^ bit) for i in range(devices)])  80.4 us
    reduce_scatter x1, waiting for transfers between devices, on_device(): lax.psum_scatter(jnp.einsum('tf,df->td', piece, w_up, preferred_element_t...  67.6 us
    reduce_scatter x1, waiting for transfers between devices, on_device(): lax.psum_scatter(jnp.dot(piece, w_out, preferred_element_type=jnp.float32...  65.3 us
    reduce_scatter x1, waiting for transfers between devices, on_device(): lax.psum_scatter(jnp.dot(piece, w_down, preferred_element_type=jnp.float3...  52.9 us
    all_gather x1, waiting for transfers between devices, on_device(): lax.all_gather(grad_hidden.astype(jnp.bfloat16), 'tensor', axis=0, tiled=...  51.8 us
    all_gather x1, waiting for transfers between devices, on_device(): full_mlp = lax.all_gather(in_mlp, 'tensor', axis=0, tiled=True)  51 us
    psum x1, blocking collectives, on_device(): lax.psum((grad_gain_attn, grad_shift_attn, grad_bias_out, grad_gain_mlp,...  44.5 us
  transfers between devices with their start and end apart: 10, of which 10 were waited for; matrix products, arithmetic and copies ran while one was open for 7% of the time, Pallas kernels for 0%

profile of v1, /device:TPU:0, one launch (start us, length us, event | category | flops | bytes accessed | tf_op | source)
XLA Modules:
  0.0 1032.9 jit_solution(17438708368219831603)
XLA Ops:
  11.4 3.2 fusion.69
  15.2 3.7 collective-permute-done
  21.3 3.7 fusion.41
  29.8 76.7 %collective-permute-done.1 = bf16[2,1176,768]{2,1,0:T(8,128)(2,1)} collective-permute-done((bf16[2,1176,768]{2,1,0:T(8,128)(2,1)}, bf16[2,1176,768]{2,1,0:T(8,128)(2,1)}, u32[]{:S(2)}, u32[]{:S(2)}) %collective-permute-start.1) | collective-permute-done | bytes 3612704 | tf_op jit(solution)/shard_map/ppermute | solution.py:23
  106.5 3.8 pad_maximum_fusion
  110.3 4.2 reverse_select_fusion
  114.5 7.2 fusion.54
  123.2 3.5 fusion.75
  126.6 6.0 convert_element_type.155
  132.7 6.4 squeeze.9
  139.1 6.5 squeeze.8
  145.6 7.4 fusion.6
  153.6 4.4 exponential_reduce_fusion
  159.1 11.1 %convert_bitcast_fusion = bf16[24,196,3,64]{1,3,2,0:T(8,128)(2,1)S(1)} fusion(f32[24,196,3,64]{1,0,3,2:T(8,128)} %squeeze.8, f32[3,64]{1,0:T(4,128)} %add.138, f32[24,3,196,196]{2,3,1,0:T(8,128)} %copy-done.2, f32[24,3,196]{2,1,0:T(4,128)S(1)} %log_add_fusion, pred[24,196]{1,0:T(8,128)(4,1)S(1)} %get-tuple-element.58), kind=kOutput, calls=%fused_computation.94 | convolution fusion | flops 367815168 | bytes 16544736 | tf_op jit(solution)/shard_map/ihqk,ikhd->iqhd/dot_general | solution.py:98
  172.9 4.8 convert_element_type.159
  177.7 6.5 convolution_convert_fusion.2
  185.7 65.3 %reduce-scatter.5.cloned.1.call-done = bf16[1176,768]{1,0:T(8,128)(2,1)} async-done(((bf16[4704,768]{1,0:T(8,128)(2,1)}), bf16[1176,768]{1,0:T(8,128)(2,1)}) %reduce-scatter.5.cloned.1.call-update) | async-done | bytes 1806352 | tf_op jit(solution)/shard_map/reduce_scatter | solution.py:104
  253.6 5.1 multiply_reduce_fusion.2
  262.4 51.0 %all-gather.4.cloned.1.call-done = bf16[4704,768]{1,0:T(8,128)(2,1)} async-done(((bf16[1176,768]{1,0:T(8,128)(2,1)}), bf16[4704,768]{1,0:T(8,128)(2,1)}) %all-gather.4.cloned.1.call-update) | async-done | bytes 7225360 | tf_op jit(solution)/shard_map/all_gather | solution.py:115
  313.4 11.8 %fusion.76 = f32[4704,768]{1,0:T(8,128)} fusion(bf16[4704,768]{1,0:T(8,128)(2,1)} %all-gather.4.cloned.1.call-done, bf16[768,768]{1,0:T(8,128)(2,1)} %param.25), kind=kOutput, calls=%fused_computation.138 | convolution fusion | flops 5549064192 | bytes 22855680 | tf_op jit(solution)/shard_map/dot_general | solution.py:116
  325.2 42.0 %all-gather.6.cloned.1.call-done = bf16[4704,768]{1,0:T(8,128)(2,1)} async-done(((bf16[1176,768]{1,0:T(8,128)(2,1)}), bf16[4704,768]{1,0:T(8,128)(2,1)}) %all-gather.6.cloned.1.call-update) | async-done | bytes 7225360 | tf_op jit(solution)/shard_map/all_gather | solution.py:132
  367.3 41.1 %fusion.70 = (f32[768]{0:T(1024)S(1)}, bf16[4704,768]{1,0:T(8,128)(2,1)}, f32[4704,768]{1,0:T(8,128)S(1)}) fusion(f32[4704,768]{1,0:T(8,128)} %fusion.76, f32[768]{0:T(1024)S(1)} %copy-done.50, bf16[4704,768]{1,0:T(8,128)(2,1)} %all-gather.6.cloned.1.call-done, bf16[768,768]{1,0:T(8,128)(2,1)S(1)} %copy-done), kind=kOutput, calls=%fused_computation.134 | convolution fusion | flops 5816400896 | bytes 44537856 | tf_op jit(solution)/shard_map/td,fd->tf/dot_general | solution.py:134
  408.4 4.5 multiply_convert_fusion.1
  412.8 10.8 %convolution_convert_fusion.1 = bf16[4704,768]{1,0:T(8,128)(2,1)} fusion(bf16[4704,768]{1,0:T(8,128)(2,1)} %multiply_convert_fusion.1, bf16[768,768]{1,0:T(8,128)(2,1)S(1)} %copy-done), kind=kOutput, calls=%fused_computation.26 | convolution fusion | flops 5552676864 | bytes 15630336 | tf_op jit(solution)/shard_map/dot_general | solution.py:121
  424.9 11.1 %convolution_convert_fusion = bf16[4704,768]{1,0:T(8,128)(2,1)} fusion(bf16[768,768]{1,0:T(8,128)(2,1)S(1)} %copy-done.54, bf16[4704,768]{1,0:T(8,128)(2,1)} %get-tuple-element.43), kind=kOutput, calls=%fused_computation.25 | convolution fusion | flops 5552676864 | bytes 15630336 | tf_op jit(solution)/shard_map/tf,df->td/dot_general | solution.py:142
  436.1 52.9 %reduce-scatter.7.cloned.1.call-done = bf16[1176,768]{1,0:T(8,128)(2,1)} async-done(((bf16[4704,768]{1,0:T(8,128)(2,1)}), bf16[1176,768]{1,0:T(8,128)(2,1)}) %reduce-scatter.7.cloned.1.call-update) | async-done | bytes 1806352 | tf_op jit(solution)/shard_map/reduce_scatter | solution.py:120
  489.0 67.6 %reduce-scatter.9.cloned.1.call-done = bf16[1176,768]{1,0:T(8,128)(2,1)} async-done(((bf16[4704,768]{1,0:T(8,128)(2,1)}), bf16[1176,768]{1,0:T(8,128)(2,1)}) %reduce-scatter.9.cloned.1.call-update) | async-done | bytes 1806352 | tf_op jit(solution)/shard_map/reduce_scatter | solution.py:141
  556.7 8.3 fusion.33
  570.6 51.8 %all-gather.8.cloned.1.call-done = bf16[4704,768]{1,0:T(8,128)(2,1)} async-done(((bf16[1176,768]{1,0:T(8,128)(2,1)}), bf16[4704,768]{1,0:T(8,128)(2,1)}) %all-gather.8.cloned.1.call-update) | async-done | bytes 7225360 | tf_op jit(solution)/shard_map/all_gather | solution.py:153
  622.4 6.8 convolution_convert_fusion.3
  629.2 6.2 reshape.197
  635.5 9.9 convert_reduce_fusion.3
  647.0 11.2 %multiply_reduce_fusion = (f32[24,3,196]{2,1,0:T(4,128)S(1)}, f32[24,3,196,196]{2,3,1,0:T(8,128)}) fusion(f32[24,3,196,196]{2,3,1,0:T(8,128)S(1)} %bitcast.89, f32[24,3,196]{2,1,0:T(4,128)S(1)} %copy-done.24, pred[24,196]{1,0:T(8,128)(4,1)S(1)} %copy-done.30, f32[24,196,3,64]{1,0,3,2:T(8,128)} %squeeze.8, f32[3,64]{1,0:T(4,128)S(1)} %copy-done.47, ...), kind=kOutput, calls=%fused_computation.2 | convolution fusion | flops 369663840 | bytes 27664992 | tf_op jit(solution)/shard_map/iqhd,ikhd->ihqk/dot_general | solution.py:171
  658.1 10.4 %multiply_convert_fusion = bf16[24,3,196,196]{2,3,1,0:T(8,128)(2,1)} fusion(f32[24,3,196,196]{2,3,1,0:T(8,128)} %get-tuple-element.63, f32[24,3,196,196]{2,3,1,0:T(8,128)S(1)} %bitcast.89, f32[24,3,196]{2,1,0:T(4,128)S(1)} %get-tuple-element.62, f32[24,3,196]{2,1,0:T(4,128)S(1)} %copy-done.24, pred[24,196]{1,0:T(8,128)(4,1)S(1)} %copy-done.30), kind=kLoop, calls=%fused_computation.1 | loop fusion | flops 16595712 | bytes 27777120 | tf_op jit(solution)/shard_map/convert_element_type | solution.py:175
  668.6 8.7 fusion.42
  683.1 4.7 convert_element_type.185
  690.6 4.7 convert_element_type.179
  698.3 3.0 convert_element_type.182
  706.5 8.0 bitcast_convert_fusion
  714.5 11.7 %fusion.35 = f32[768,768]{1,0:T(8,128)} fusion(bf16[4704,768]{1,0:T(8,128)(2,1)} %all-gather.4.cloned.1.call-done, bf16[4704,768]{1,0:T(8,128)(2,1)} %get-tuple-element.43), kind=kOutput, calls=%fused_computation.79 | convolution fusion | flops 5549064192 | bytes 16809984 | tf_op jit(solution)/shard_map/td,tf->df/dot_general | solution.py:139
  726.3 12.2 %fusion.78 = f32[768,768]{1,0:T(8,128)} fusion(bf16[4704,768]{1,0:T(8,128)(2,1)} %multiply_convert_fusion.1, bf16[4704,768]{1,0:T(8,128)(2,1)} %all-gather.6.cloned.1.call-done), kind=kOutput, calls=%fused_computation.140 | convolution fusion | flops 5549064192 | bytes 16809984 | tf_op jit(solution)/shard_map/tf,td->fd/dot_general | solution.py:133
  741.0 5.9 fusion.8
  749.9 22.2 %all-reduce.1 = (f32[2,192]{1,0:T(2,128)}, f32[768]{0:T(1024)}) all-reduce(f32[2,192]{1,0:T(2,128)S(1)} %pad_maximum_fusion.2, f32[768]{0:T(1024)S(1)} %get-tuple-element.42), channel_id=1, replica_groups=mesh['dp'=8,'tensor'=4] {'dp'}, use_global_device_ids=true, to_apply=%region_22.23 | all-reduce | flops 1152 | bytes 9216 | tf_op jit(solution)/shard_map/psum | solution.py:227
  772.2 7.6 reduce-scatter.11.cloned.1.call-done
  779.8 3.4 fusion.34
  783.2 44.5 %all-reduce = (f32[768]{0:T(1024)}, f32[768]{0:T(1024)}, f32[768]{0:T(1024)}, f32[768]{0:T(1024)}, f32[768]{0:T(1024)}, /*index=5*/f32[768]{0:T(1024)}, f32[4]{0:T(128)S(1)}) all-reduce(f32[768]{0:T(1024)S(1)} %get-tuple-element.17, f32[768]{0:T(1024)S(1)} %get-tuple-element.25, ...), channel_id=1, replica_groups=mesh['dp'=8,'tensor'=4] {'dp','tensor'}, use_global_device_ids=true, to_apply=%region_16.17 | all-reduce | flops 4612 | bytes 36896 | tf_op jit(solution)/shard_map/psum | solution.py:215
  829.5 4.6 fusion.26
  834.1 183.9 %all-reduce.5.cloned.1.call-done = (f32[768,3,192]{0,2,1:T(8,128)}, f32[192,768]{1,0:T(8,128)}, f32[768,768]{1,0:T(8,128)}, f32[768,768]{1,0:T(8,128)}) async-done(((f32[768,3,192]{0,2,1:T(8,128)}, f32[192,768]{1,0:T(8,128)}, f32[768,768]{1,0:T(8,128)}, f32[768,768]{1,0:T(8,128)}), (f32[768,3,192]{0,2,1:T(8,128)}, f32[192,768]{1,0:T(8,128)}, f32[768,768]{1,0:T(8,128)}, ...) | async-done | bytes 7077904 | tf_op jit(solution)/shard_map/psum | solution.py:227
  (201 shorter events, 65.2 us)
Async XLA Ops:
  7.2 360.1 %copy-start = (bf16[768,768]{1,0:T(8,128)(2,1)S(1)}, bf16[768,768]{1,0:T(8,128)(2,1)}, u32[]{:S(2)}) copy-start(bf16[768,768]{1,0:T(8,128)(2,1)} %param.27) | copy-start | bytes 3538948
  7.2 243.8 %reduce-scatter.5.cloned.1.call-start = ((), (), s32[]{:S(2)}) async-start(), calls=%async_computation.4 | async-start | bytes 9031680 | tf_op jit(solution)/shard_map/reduce_scatter | solution.py:104
  14.7 4.2 collective-permute-start
  25.0 81.6 %collective-permute-start.1 = (bf16[2,1176,768]{2,1,0:T(8,128)(2,1)}, bf16[2,1176,768]{2,1,0:T(8,128)(2,1)}, u32[]{:S(2)}, u32[]{:S(2)}) collective-permute-start(bf16[2,1176,768]{2,1,0:T(8,128)(2,1)} %get-tuple-element.53), channel_id=1, source_target_pairs={{0,2},{1,3},{2,0},{3,1},{4,6},{5,7},{6,4},{7,5},{8,10},{9,11},{10,... | collective-permute-start | bytes 10838024 | tf_op jit(solution)/shard_map/ppermute | solution.py:23
  29.8 129.2 %copy-start.29 = (pred[24,196]{1,0:T(8,128)(4,1)}, pred[24,196]{1,0:T(8,128)(4,1)S(1)}, u32[]{:S(2)}) copy-start(pred[24,196]{1,0:T(8,128)(4,1)S(1)} %get-tuple-element.58) | copy-start | bytes 14116
  159.0 11.1 %copy-start.23 = (f32[24,3,196]{2,1,0:T(4,128)}, f32[24,3,196]{2,1,0:T(4,128)S(1)}, u32[]{:S(2)}) copy-start(f32[24,3,196]{2,1,0:T(4,128)S(1)} %log_add_fusion) | copy-start | bytes 169348
  184.2 66.8 %copy-start.41 = (f32[768]{0:T(1024)S(1)}, f32[768]{0:T(1024)}, u32[]{:S(2)}) copy-start(f32[768]{0:T(1024)} %param.22) | copy-start | bytes 9220
  184.2 129.2 %all-gather.4.cloned.1.call-start = ((), (), s32[]{:S(2)}) async-start(), calls=%async_computation.5 | async-start | bytes 9031680 | tf_op jit(solution)/shard_map/all_gather | solution.py:115
  185.7 73.0 %copy-start.37 = (f32[1176]{0:T(1024)}, f32[1176]{0:T(1024)S(1)}, u32[]{:S(2)}) copy-start(f32[1176]{0:T(1024)S(1)} %get-tuple-element.46) | copy-start | bytes 14116
  185.7 73.6 %copy-start.44 = (f32[768]{0:T(1024)S(1)}, f32[768]{0:T(1024)}, u32[]{:S(2)}) copy-start(f32[768]{0:T(1024)} %param.23) | copy-start | bytes 9220
  185.7 73.6 %copy-start.52 = (f32[768]{0:T(1024)S(1)}, f32[768]{0:T(1024)}, u32[]{:S(2)}) copy-start(f32[768]{0:T(1024)} %param.24) | copy-start | bytes 9220
  261.6 105.6 %all-gather.6.cloned.1.call-start = ((), (), s32[]{:S(2)}) async-start(), calls=%async_computation.7 | async-start | bytes 9031680 | tf_op jit(solution)/shard_map/all_gather | solution.py:132
  262.4 104.9 %copy-start.50 = (f32[768]{0:T(1024)S(1)}, f32[768]{0:T(1024)}, u32[]{:S(2)}) copy-start(f32[768]{0:T(1024)} %param.26) | copy-start | bytes 9220
  262.4 226.6 %reduce-scatter.7.cloned.1.call-start = ((), (), s32[]{:S(2)}) async-start(), calls=%async_computation.6 | async-start | bytes 9031680 | tf_op jit(solution)/shard_map/reduce_scatter | solution.py:120
  367.3 41.1 %copy-start.13 = (f32[4704,768]{1,0:T(8,128)S(1)}, f32[4704,768]{1,0:T(8,128)}, u32[]{:S(2)}) copy-start(f32[4704,768]{1,0:T(8,128)} %fusion.76) | copy-start | bytes 43352068
  423.7 132.9 %reduce-scatter.9.cloned.1.call-start = ((), (), s32[]{:S(2)}) async-start(), calls=%async_computation.8 | async-start | bytes 9031680 | tf_op jit(solution)/shard_map/reduce_scatter | solution.py:141
  436.0 120.6 %copy-start.4 = (bf16[1176,768]{1,0:T(8,128)(2,1)S(1)}, bf16[1176,768]{1,0:T(8,128)(2,1)}, u32[]{:S(2)}) copy-start(bf16[1176,768]{1,0:T(8,128)(2,1)} %param.15) | copy-start | bytes 5419012
  436.0 120.6 %copy-start.34 = (f32[1176]{0:T(1024)S(1)}, f32[1176]{0:T(1024)}, u32[]{:S(2)}) copy-start(f32[1176]{0:T(1024)} %copy-done.33) | copy-start | bytes 14116
  436.0 120.6 %copy-start.38 = (f32[1176]{0:T(1024)S(1)}, f32[1176]{0:T(1024)}, u32[]{:S(2)}) copy-start(f32[1176]{0:T(1024)} %copy-done.37) | copy-start | bytes 14116
  436.0 120.6 %copy-start.40 = (f32[1176]{0:T(1024)S(1)}, f32[1176]{0:T(1024)}, u32[]{:S(2)}) copy-start(f32[1176]{0:T(1024)} %copy-done.39) | copy-start | bytes 14116
  436.0 120.6 %copy-start.42 = (f32[768]{0:T(1024)S(1)}, f32[768]{0:T(1024)}, u32[]{:S(2)}) copy-start(f32[768]{0:T(1024)} %param.22) | copy-start | bytes 9220
  436.0 120.6 %copy-start.45 = (f32[768]{0:T(1024)S(1)}, f32[768]{0:T(1024)}, u32[]{:S(2)}) copy-start(f32[768]{0:T(1024)} %param.23) | copy-start | bytes 9220
  436.0 120.6 %copy-start.51 = (f32[768]{0:T(1024)S(1)}, f32[768]{0:T(1024)}, u32[]{:S(2)}) copy-start(f32[768]{0:T(1024)} %param.28) | copy-start | bytes 9220
  436.0 186.3 %all-gather.8.cloned.1.call-start = ((), (), s32[]{:S(2)}) async-start(), calls=%async_computation.9 | async-start | bytes 9031680 | tf_op jit(solution)/shard_map/all_gather | solution.py:153
  567.3 55.1 %copy-start.28 = (bf16[192,768]{1,0:T(8,128)(2,1)S(1)}, bf16[192,768]{1,0:T(8,128)(2,1)}, u32[]{:S(2)}) copy-start(bf16[192,768]{1,0:T(8,128)(2,1)} %param.21) | copy-start | bytes 884740
  570.6 64.8 %copy-start.24 = (f32[24,3,196]{2,1,0:T(4,128)S(1)}, f32[24,3,196]{2,1,0:T(4,128)}, u32[]{:S(2)}) copy-start(f32[24,3,196]{2,1,0:T(4,128)} %copy-done.23) | copy-start | bytes 169348
  570.6 64.8 %copy-start.30 = (pred[24,196]{1,0:T(8,128)(4,1)S(1)}, pred[24,196]{1,0:T(8,128)(4,1)}, u32[]{:S(2)}) copy-start(pred[24,196]{1,0:T(8,128)(4,1)} %copy-done.29) | copy-start | bytes 14116
  570.6 209.2 %reduce-scatter.11.cloned.1.call-start = ((), (), s32[]{:S(2)}) async-start(), calls=%async_computation.10 | async-start | bytes 9031680 | tf_op jit(solution)/shard_map/reduce_scatter | solution.py:196
  629.2 16.2 %slice-start = ((s8[14745600]{0:T(1024)(128)(4,1)}), s8[2162688]{0:T(1024)(128)(4,1)S(1)}, s32[]{:S(2)}) async-start(s8[14745600]{0:T(1024)(128)(4,1)} %bitcast.88), calls=%async_computation.12 | async-start | bytes 4325376
  635.4 10.0 slice-start.1
  635.4 10.0 slice-start.2
  635.4 10.9 %slice-start.3 = ((s8[14745600]{0:T(1024)(128)(4,1)}), s8[4194304]{0:T(1024)(128)(4,1)S(1)}, s32[]{:S(2)}) async-start(s8[14745600]{0:T(1024)(128)(4,1)} %bitcast.88), calls=%async_computation.15 | async-start | bytes 8388608
  635.4 11.5 %copy-start.11 = (bf16[24,196,3,64]{1,0,3,2:T(8,128)(2,1)S(1)}, bf16[24,196,3,64]{1,0,3,2:T(8,128)(2,1)}, u32[]{:S(2)}) copy-start(bf16[24,196,3,64]{1,0,3,2:T(8,128)(2,1)} %reshape.197) | copy-start | bytes 5419012
  635.4 11.5 %copy-start.47 = (f32[3,64]{1,0:T(4,128)S(1)}, f32[3,64]{1,0:T(4,128)}, u32[]{:S(2)}) copy-start(f32[3,64]{1,0:T(4,128)} %add.138) | copy-start | bytes 2308
  658.1 10.4 %copy-start.48 = (f32[3,64]{1,0:T(4,128)S(1)}, f32[3,64]{1,0:T(4,128)}, u32[]{:S(2)}) copy-start(f32[3,64]{1,0:T(4,128)} %add.141) | copy-start | bytes 2308
  714.5 303.6 %all-reduce.5.cloned.1.call-start = ((), (), s32[]{:S(2)}) async-start(), calls=%async_computation.11 | async-start | bytes 14155776 | tf_op jit(solution)/shard_map/psum | solution.py:227
  714.5 23.9 %slice-start.8 = ((s8[7225344]{0:T(1024)(128)(4,1)}), s8[4194304]{0:T(1024)(128)(4,1)S(1)}, s32[]{:S(2)}) async-start(s8[7225344]{0:T(1024)(128)(4,1)} %bitcast.98), calls=%async_computation.20 | async-start | bytes 8388608
  714.5 26.5 %slice-start.4 = ((s8[7225344]{0:T(1024)(128)(4,1)}), s8[4194304]{0:T(1024)(128)(4,1)S(1)}, s32[]{:S(2)}) async-start(s8[7225344]{0:T(1024)(128)(4,1)} %bitcast.92), calls=%async_computation.16 | async-start | bytes 8388608
  714.5 26.5 %slice-start.6 = ((s8[5455872]{0:T(1024)(128)(4,1)}), s8[4194304]{0:T(1024)(128)(4,1)S(1)}, s32[]{:S(2)}) async-start(s8[5455872]{0:T(1024)(128)(4,1)} %bitcast.96), calls=%async_computation.18 | async-start | bytes 8388608
  726.3 12.2 %copy-start.14 = (bf16[4704,192]{0,1:T(8,128)(2,1)S(1)}, bf16[4704,192]{0,1:T(8,128)(2,1)}, u32[]{:S(2)}) copy-start(bf16[4704,192]{0,1:T(8,128)(2,1)} %convert_element_type.159) | copy-start | bytes 5419012
  726.3 12.2 %slice-start.9 = ((s8[7225344]{0:T(1024)(128)(4,1)}), s8[3031040]{0:T(1024)(128)(4,1)S(1)}, s32[]{:S(2)}) async-start(s8[7225344]{0:T(1024)(128)(4,1)} %bitcast.98), calls=%async_computation.21 | async-start | bytes 6062080
  726.3 14.7 %slice-start.5 = ((s8[7225344]{0:T(1024)(128)(4,1)}), s8[3031040]{0:T(1024)(128)(4,1)S(1)}, s32[]{:S(2)}) async-start(s8[7225344]{0:T(1024)(128)(4,1)} %bitcast.92), calls=%async_computation.17 | async-start | bytes 6062080
  726.3 14.7 %slice-start.7 = ((s8[5455872]{0:T(1024)(128)(4,1)}), s8[1261568]{0:T(1024)(128)(4,1)S(1)}, s32[]{:S(2)}) async-start(s8[5455872]{0:T(1024)(128)(4,1)} %bitcast.96), calls=%async_computation.19 | async-start | bytes 2523136
  746.9 32.9 %copy-start.5 = (bf16[1176,768]{1,0:T(8,128)(2,1)S(1)}, bf16[1176,768]{1,0:T(8,128)(2,1)}, u32[]{:S(2)}) copy-start(bf16[1176,768]{1,0:T(8,128)(2,1)} %param.15) | copy-start | bytes 5419012
  746.9 32.9 %copy-start.32 = (f32[1176]{0:T(1024)S(1)}, f32[1176]{0:T(1024)}, u32[]{:S(2)}) copy-start(f32[1176]{0:T(1024)} %copy-done.31) | copy-start | bytes 14116
  746.9 32.9 %copy-start.36 = (f32[1176]{0:T(1024)S(1)}, f32[1176]{0:T(1024)}, u32[]{:S(2)}) copy-start(f32[1176]{0:T(1024)} %copy-done.35) | copy-start | bytes 14116
  746.9 32.9 %copy-start.46 = (f32[768]{0:T(1024)S(1)}, f32[768]{0:T(1024)}, u32[]{:S(2)}) copy-start(f32[768]{0:T(1024)} %param.17) | copy-start | bytes 9220
  746.9 36.3 %copy-start.49 = (f32[768]{0:T(1024)S(1)}, f32[768]{0:T(1024)}, u32[]{:S(2)}) copy-start(f32[768]{0:T(1024)} %get-tuple-element.26) | copy-start | bytes 9220
  (30 other events, 137.6 us)
Sparse Core Ops, SparseCore 0:
  184.4 66.6 reduce-scatter.4
  261.8 51.6 all-gather.3
  315.6 51.6 all-gather.5
  423.8 65.1 reduce-scatter.6
  491.4 65.1 reduce-scatter.8
  570.7 51.6 all-gather.7
  714.6 65.1 reduce-scatter.10
  785.4 232.6 all-reduce.4
